TPU v7x, 32 devices: a whole 2x2x4 slice. The times are simulated.
32 devices in a mesh: bits: 16 (over z, y, x), docs: 2 (over core).
Axes of the slice: x: 2, y: 2, z: 4, core: 2. Of those that a mesh axis runs over, the one named last changes fastest.
Arguments:
- positions: int32 [1024, 4096], P(('bits', 'docs')), may hold values from 0 to 4095
- element_weights: float32 [1024, 1024], P(('bits', 'docs')), may hold values from 0.25 to 4
- set_sizes: int32 [1024], P(('bits', 'docs')), may hold values from 256 to 1024, as said below
- bit_weights: bfloat16 [4096], replicated, may hold values from 0.25 to 4
- candidates: int32 [2, 16, 16], P('docs'), may hold values from 0 to 63, as said below
Outputs:
- scores: float32 [2, 16, 128, 64], P('docs', 'bits')
Inputs may be any that keep to these rules, and one draw needn't show every extreme that they name: `set_sizes`: one document in every draw has exactly 1024 elements. `candidates`: the 16 row tiles named for one block are distinct. `positions`: entries of a row beyond its first 4 * set_sizes are not part of the filter.
All inputs are finite; a program needn't handle non-finite values.
Results may differ from a plain program's by a relative error of at most 0.0012.
Values may be sent and summed in bfloat16 or wider, within the bound.
A program may use at most 64 MiB of HBM per device.

v0:
```python
import math
import jax
import jax.numpy as jnp
from jax import lax
from jax.sharding import PartitionSpec as P

FILTER_BITS = 4096
HASHES = 4
TILE = 8


def build_filter(positions, element_weights, set_sizes):
    doc_count, slot_count = positions.shape
    elem_count = element_weights.shape[1]
    low_cells = 64
    high_cells = FILTER_BITS // low_cells
    slot_index = jnp.arange(slot_count, dtype=jnp.int32)
    usable = slot_index[None, :] < HASHES * set_sizes[:, None]
    spread = jnp.broadcast_to(element_weights[:, :, None], (doc_count, elem_count, HASHES)).reshape(
        doc_count, slot_count
    )
    slot_weights = jnp.where(usable, spread, 0.0)
    upper = slot_weights.astype(jnp.bfloat16)
    remain = slot_weights - upper.astype(jnp.float32)
    middle = remain.astype(jnp.bfloat16)
    lower = (remain - middle.astype(jnp.float32)).astype(jnp.bfloat16)
    weight_parts = jnp.stack([upper, middle, lower], axis=1)
    high_index = positions // low_cells
    low_index = positions - high_index * low_cells
    group = math.gcd(doc_count, 8)

    def one_group(inputs):
        part_block, high_block, low_block = inputs
        high_onehot = (high_block[:, :, None] == jnp.arange(high_cells, dtype=jnp.int32)).astype(
            jnp.bfloat16
        )
        low_onehot = (low_block[:, :, None] == jnp.arange(low_cells, dtype=jnp.int32)).astype(
            jnp.bfloat16
        )
        left = part_block[:, :, :, None] * high_onehot[:, None, :, :]
        summed = jnp.einsum("dcph,dpl->dhl", left, low_onehot, preferred_element_type=jnp.float32)
        return summed.reshape(group, FILTER_BITS)

    grouped = lax.map(
        one_group,
        (
            weight_parts.reshape(doc_count // group, group, 3, slot_count),
            high_index.reshape(doc_count // group, group, slot_count),
            low_index.reshape(doc_count // group, group, slot_count),
        ),
    )
    return grouped.reshape(doc_count, FILTER_BITS).astype(jnp.bfloat16)


def weighted_pop(cells, weights):
    weighted = cells * weights
    return jnp.sum(weighted.astype(jnp.float32) * cells.astype(jnp.float32), axis=1)


def estimate(shared, pop_rows, pop_cols, size_rows, size_cols):
    union_weight = pop_rows[:, None] + pop_cols[None, :] - shared
    ratio = shared / union_weight
    smaller = jnp.minimum(size_rows[:, None], size_cols[None, :])
    return ratio * (size_rows[:, None] + size_cols[None, :]) / ((1.0 + ratio) * smaller)


def pick_tiles(slice_cells, tile_choice, row_group, groups, row_half):
    width = slice_cells.shape[1]
    row_tiles = row_half // TILE
    tiles = slice_cells.reshape(groups, row_tiles, TILE * width)
    own_tiles = lax.dynamic_index_in_dim(tiles, row_group, 0, keepdims=False)
    onehot = (tile_choice[:, :, None] == jnp.arange(row_tiles, dtype=jnp.int32)).astype(
        jnp.bfloat16
    )
    picked = jnp.einsum("jcr,rw->jcw", onehot, own_tiles, preferred_element_type=jnp.float32)
    return picked.astype(jnp.bfloat16).reshape(
        tile_choice.shape[0], tile_choice.shape[1] * TILE, width
    )


def body(positions, element_weights, set_sizes, bit_weights, candidates):
    col_index = lax.axis_index("bits")
    row_group = lax.axis_index("docs")
    blocks = lax.axis_size("bits")
    groups = lax.axis_size("docs")
    doc_total = positions.shape[0] * blocks * groups
    row_half = doc_total // groups
    col_width = doc_total // blocks
    slot_count = candidates.shape[2] * TILE
    tile_offsets = jnp.arange(TILE, dtype=jnp.int32)
    own_cells = build_filter(positions, element_weights, set_sizes)
    local_pop = weighted_pop(own_cells, bit_weights)
    every_pop, size_float = (
        lax.all_gather(local_pop, ("bits", "docs"), axis=0, tiled=True),
        lax.all_gather(set_sizes.astype(jnp.float32), ("bits", "docs"), axis=0, tiled=True),
    )
    pair_cells = lax.all_gather(own_cells, "docs", axis=0, tiled=True)
    slice_cells = lax.all_to_all(pair_cells, "bits", split_axis=1, concat_axis=0, tiled=True)
    tile_rows = row_group * row_half + (candidates[0][:, :, None] * TILE + tile_offsets).reshape(
        blocks, slot_count
    )
    picked_cells = pick_tiles(slice_cells, candidates[0], row_group, groups, row_half)
    row_cells = lax.all_to_all(picked_cells, "bits", split_axis=0, concat_axis=2, tiled=True)[0]
    shared = lax.dot_general(
        row_cells * bit_weights,
        pair_cells,
        (((1,), (1,)), ((), ())),
        preferred_element_type=jnp.float32,
    )
    row_docs = lax.dynamic_index_in_dim(tile_rows, col_index, 0, keepdims=False)
    pop_rows = every_pop[row_docs]
    pop_cols = lax.dynamic_slice_in_dim(every_pop, col_index * col_width, col_width, 0)
    size_rows = size_float[row_docs]
    size_cols = lax.dynamic_slice_in_dim(size_float, col_index * col_width, col_width, 0)
    scores = estimate(shared, pop_rows, pop_cols, size_rows, size_cols)
    return scores.reshape(1, 1, slot_count, col_width)


def solution(mesh):
    return jax.shard_map(
        body,
        mesh=mesh,
        in_specs=(
            P(("bits", "docs"), None),
            P(("bits", "docs"), None),
            P(("bits", "docs")),
            P(),
            P("docs", None, None),
        ),
        out_specs=P("docs", "bits", None, None),
        check_vma=False,
    )
```

profile of v0, /device:TPU:0, one launch (start us, length us, event | category | flops | bytes accessed | tf_op | source)
XLA Modules:
  0.0 158.0 jit_solution(18137033540736739117)
XLA Ops:
  0.0 1.1 copy.33
  1.1 0.4 broadcast_in_dim.12
  1.5 5.7 %reshape.175 = f32[4,8,1,4096]{1,0,3,2:T(4,128)} reshape(f32[32,1024,4]{0,2,1:T(4,128)S(1)} %broadcast_in_dim.12) | data formatting | bytes 1048576 | tf_op jit(solution)/shard_map/reshape | solution.py:19
  7.2 6.7 %copy.34 = f32[4,8,1,4096]{3,1,2,0:T(8,128)S(1)} copy(f32[4,8,1,4096]{1,0,3,2:T(4,128)} %reshape.175) | data formatting | bytes 1048576 | tf_op jit(solution)/shard_map/reshape | solution.py:19
  14.3 0.3 subtract_bitcast_fusion
  14.7 60.3 %while.10 = (s32[]{:T(128)}, bf16[4,8,4096]{2,1,0:T(8,128)(2,1)S(1)}, bf16[4,8,3,4096]{3,1,2,0:T(8,128)(2,1)S(1)}, s32[4,8,4096]{2,1,0:T(8,128)S(1)}, s32[4,8,4096]{2,1,0:T(8,128)S(1)}, /*index=5*/s32[]{:T(128)}) while((s32[]{:T(128)}, bf16[4,8,4096]{2,1,0:T(8,128)(2,1)S(1)}, bf16[4,8,3,4096]{3,1,2,0:T(8,128)(2,1)S(1)}, ...), condition=%wide.region_2.3_spmd, body=%wide.region_0.2_spmd.sunk | while | flops 304087040 | bytes 18874448 | solution.py:44
  14.8 3.0 %fusion.23 = bf16[8,4096,64]{1,2,0:T(8,128)(2,1)} fusion(s32[8,4096]{1,0:T(8,128)S(1)} %get-tuple-element.109), kind=kLoop, calls=%fused_computation.5.clone.1 | loop fusion | flops 4194304 | bytes 4325376 | tf_op jit(solution)/shard_map/while/body/eval_jaxpr/convert_element_type | solution.py:34
  18.0 7.9 %convert_reduce_fusion.2 = bf16[8,4096,64]{1,2,0:T(8,128)(2,1)} fusion(bf16[8,4096,64]{1,2,0:T(8,128)(2,1)} %fusion.23, bf16[8,3,4096]{2,1,0:T(4,128)(2,1)S(1)} %bitcast.50), kind=kLoop, calls=%fused_computation.2.clone.1 | loop fusion | flops 29360128 | bytes 8585216 | tf_op jit(solution)/shard_map/while/body/eval_jaxpr/dcph,dpl->dhl/reduce_sum | solution.py:41
  25.9 3.7 %fusion.24 = bf16[8,64,64]{2,1,0:T(8,128)(2,1)S(1)} fusion(bf16[8,4096,64]{1,2,0:T(8,128)(2,1)} %convert_reduce_fusion.2, s32[8,4096]{1,0:T(8,128)S(1)} %get-tuple-element.110), kind=kOutput, calls=%fused_computation.6.clone.1 | convolution fusion | flops 270532608 | bytes 4390912 | tf_op jit(solution)/shard_map/while/body/eval_jaxpr/dcph,dpl->dhl/dot_general | solution.py:41
  29.8 3.0 %fusion.23 = bf16[8,4096,64]{1,2,0:T(8,128)(2,1)} fusion(s32[8,4096]{1,0:T(8,128)S(1)} %get-tuple-element.109), kind=kLoop, calls=%fused_computation.5.clone.1 | loop fusion | flops 4194304 | bytes 4325376 | tf_op jit(solution)/shard_map/while/body/eval_jaxpr/convert_element_type | solution.py:34
  33.1 7.9 %convert_reduce_fusion.2 = bf16[8,4096,64]{1,2,0:T(8,128)(2,1)} fusion(bf16[8,4096,64]{1,2,0:T(8,128)(2,1)} %fusion.23, bf16[8,3,4096]{2,1,0:T(4,128)(2,1)S(1)} %bitcast.50), kind=kLoop, calls=%fused_computation.2.clone.1 | loop fusion | flops 29360128 | bytes 8585216 | tf_op jit(solution)/shard_map/while/body/eval_jaxpr/dcph,dpl->dhl/reduce_sum | solution.py:41
  40.9 3.7 %fusion.24 = bf16[8,64,64]{2,1,0:T(8,128)(2,1)S(1)} fusion(bf16[8,4096,64]{1,2,0:T(8,128)(2,1)} %convert_reduce_fusion.2, s32[8,4096]{1,0:T(8,128)S(1)} %get-tuple-element.110), kind=kOutput, calls=%fused_computation.6.clone.1 | convolution fusion | flops 270532608 | bytes 4390912 | tf_op jit(solution)/shard_map/while/body/eval_jaxpr/dcph,dpl->dhl/dot_general | solution.py:41
  44.9 3.0 %fusion.23 = bf16[8,4096,64]{1,2,0:T(8,128)(2,1)} fusion(s32[8,4096]{1,0:T(8,128)S(1)} %get-tuple-element.109), kind=kLoop, calls=%fused_computation.5.clone.1 | loop fusion | flops 4194304 | bytes 4325376 | tf_op jit(solution)/shard_map/while/body/eval_jaxpr/convert_element_type | solution.py:34
  48.1 7.9 %convert_reduce_fusion.2 = bf16[8,4096,64]{1,2,0:T(8,128)(2,1)} fusion(bf16[8,4096,64]{1,2,0:T(8,128)(2,1)} %fusion.23, bf16[8,3,4096]{2,1,0:T(4,128)(2,1)S(1)} %bitcast.50), kind=kLoop, calls=%fused_computation.2.clone.1 | loop fusion | flops 29360128 | bytes 8585216 | tf_op jit(solution)/shard_map/while/body/eval_jaxpr/dcph,dpl->dhl/reduce_sum | solution.py:41
  56.0 3.7 %fusion.24 = bf16[8,64,64]{2,1,0:T(8,128)(2,1)S(1)} fusion(bf16[8,4096,64]{1,2,0:T(8,128)(2,1)} %convert_reduce_fusion.2, s32[8,4096]{1,0:T(8,128)S(1)} %get-tuple-element.110), kind=kOutput, calls=%fused_computation.6.clone.1 | convolution fusion | flops 270532608 | bytes 4390912 | tf_op jit(solution)/shard_map/while/body/eval_jaxpr/dcph,dpl->dhl/dot_general | solution.py:41
  60.0 3.0 %fusion.23 = bf16[8,4096,64]{1,2,0:T(8,128)(2,1)} fusion(s32[8,4096]{1,0:T(8,128)S(1)} %get-tuple-element.109), kind=kLoop, calls=%fused_computation.5.clone.1 | loop fusion | flops 4194304 | bytes 4325376 | tf_op jit(solution)/shard_map/while/body/eval_jaxpr/convert_element_type | solution.py:34
  63.2 7.9 %convert_reduce_fusion.2 = bf16[8,4096,64]{1,2,0:T(8,128)(2,1)} fusion(bf16[8,4096,64]{1,2,0:T(8,128)(2,1)} %fusion.23, bf16[8,3,4096]{2,1,0:T(4,128)(2,1)S(1)} %bitcast.50), kind=kLoop, calls=%fused_computation.2.clone.1 | loop fusion | flops 29360128 | bytes 8585216 | tf_op jit(solution)/shard_map/while/body/eval_jaxpr/dcph,dpl->dhl/reduce_sum | solution.py:41
  71.1 3.7 %fusion.24 = bf16[8,64,64]{2,1,0:T(8,128)(2,1)S(1)} fusion(bf16[8,4096,64]{1,2,0:T(8,128)(2,1)} %convert_reduce_fusion.2, s32[8,4096]{1,0:T(8,128)S(1)} %get-tuple-element.110), kind=kOutput, calls=%fused_computation.6.clone.1 | convolution fusion | flops 270532608 | bytes 4390912 | tf_op jit(solution)/shard_map/while/body/eval_jaxpr/dcph,dpl->dhl/dot_general | solution.py:41
  75.0 2.3 %all_gather.9 = bf16[64,4096]{1,0:T(8,128)(2,1)S(1)} all-gather(bf16[32,4096]{1,0:T(8,128)(2,1)S(1)} %bitcast.53), channel_id=1, replica_groups=mesh['bits'=16,'docs'=2] {'docs'}, dimensions={0}, use_global_device_ids=true | all-gather | bytes 786432 | tf_op jit(solution)/shard_map/all_gather | solution.py:97
  77.3 0.8 copy.44
  78.1 8.3 %all-to-all-start = ((bf16[64,16,256]{2,0,1:T(8,128)(2,1)}), bf16[64,16,256]{2,0,1:T(8,128)(2,1)S(1)}, u32[]{:S(2)}, u32[]{:S(2)}) async-start(bf16[64,16,256]{2,0,1:T(8,128)(2,1)} %bitcast.43), calls=%async_computation | async-start | bytes 1048576 | tf_op jit(solution)/shard_map/all_to_all | solution.py:98
  86.4 15.4 %all-to-all-done = bf16[64,16,256]{2,0,1:T(8,128)(2,1)S(1)} async-done(((bf16[64,16,256]{2,0,1:T(8,128)(2,1)}), bf16[64,16,256]{2,0,1:T(8,128)(2,1)S(1)}, u32[]{:S(2)}, u32[]{:S(2)}) %all-to-all-start) | async-done | bytes 524320 | tf_op jit(solution)/shard_map/all_to_all | solution.py:98
  101.8 0.2 reshape.178
  102.0 0.5 convolution_convert_fusion
  102.5 0.5 reshape.179
  103.1 1.3 copy.37
  104.4 3.9 %all-to-all-start.1 = ((bf16[16,128,256]{1,2,0:T(8,128)(2,1)}), bf16[16,128,256]{1,2,0:T(8,128)(2,1)S(1)}, u32[]{:S(2)}, u32[]{:S(2)}) async-start(bf16[16,128,256]{1,2,0:T(8,128)(2,1)} %copy.37), calls=%async_computation.1 | async-start | bytes 2097152 | tf_op jit(solution)/shard_map/all_to_all | solution.py:103
  108.9 44.8 %all-reduce.2 = (f32[1024]{0:T(1024)S(1)}, f32[1024]{0:T(1024)S(1)}) all-reduce(f32[1024]{0:T(1024)S(1)} %convert_dynamic-update-slice_fusion, f32[1024]{0:T(1024)S(1)} %dynamic-update-slice), channel_id=1, replica_groups=mesh['bits'=16,'docs'=2] {'bits','docs'}, use_global_device_ids=true, to_apply=%add.1 | all-reduce | flops 2048 | bytes 16384
  154.2 1.0 gather_fusion
  155.2 1.0 gather_fusion.1
  156.2 0.8 bitcast_multiply_fusion
  157.0 1.0 divide_bitcast_fusion
  (51 shorter events, 3.1 us)
Async XLA Ops:
  7.2 6.7 %copy-start.3 = (s32[32]{0:T(128)S(1)}, s32[32]{0:T(128)}, u32[]{:S(2)}) copy-start(s32[32]{0:T(128)} %param.9) | copy-start | bytes 388
  7.2 7.1 %copy-start = (s32[32,4096]{1,0:T(8,128)S(1)}, s32[32,4096]{1,0:T(8,128)}, u32[]{:S(2)}) copy-start(s32[32,4096]{1,0:T(8,128)} %param.7) | copy-start | bytes 1572868
  14.7 87.3 %copy-start.2 = (s32[1,16,16]{2,1,0:T(8,128)S(1)}, s32[1,16,16]{2,1,0:T(8,128)}, u32[]{:S(2)}) copy-start(s32[1,16,16]{2,1,0:T(8,128)} %param.11) | copy-start | bytes 3076
  78.1 23.6 %all-to-all-start = ((bf16[64,16,256]{2,0,1:T(8,128)(2,1)}), bf16[64,16,256]{2,0,1:T(8,128)(2,1)S(1)}, u32[]{:S(2)}, u32[]{:S(2)}) async-start(bf16[64,16,256]{2,0,1:T(8,128)(2,1)} %bitcast.43), calls=%async_computation | async-start | bytes 1048576 | tf_op jit(solution)/shard_map/all_to_all | solution.py:98
  101.8 6.5 %copy-start.1 = (bf16[4096]{0:T(1024)(128)(2,1)S(1)}, bf16[4096]{0:T(1024)(128)(2,1)}, u32[]{:S(2)}) copy-start(bf16[4096]{0:T(1024)(128)(2,1)} %param.10) | copy-start | bytes 24580
  104.4 51.8 %all-to-all-start.1 = ((bf16[16,128,256]{1,2,0:T(8,128)(2,1)}), bf16[16,128,256]{1,2,0:T(8,128)(2,1)S(1)}, u32[]{:S(2)}, u32[]{:S(2)}) async-start(bf16[16,128,256]{1,2,0:T(8,128)(2,1)} %copy.37), calls=%async_computation.1 | async-start | bytes 2097152 | tf_op jit(solution)/shard_map/all_to_all | solution.py:103
where the time goes:
time: 159 us; the launch traced here: 158 us
  blocking collectives  47.1 us (30%)
  other arithmetic  45.5 us (29%)
  local copies, waits for them, and re-layouts  21 us (13%)
  matrix products  16.3 us (10%)
  waiting for transfers between devices  15.4 us (10%)
  starting transfers between devices  12.2 us (8%)
    unnamed x1, blocking collectives  44.8 us
    reduce_sum x4, other arithmetic, one_group(): jnp.einsum('dcph,dpl->dhl', left, low_onehot, preferred_element_type=jnp....  31.4 us
    all_to_all x1, waiting for transfers between devices, body(): lax.all_to_all(pair_cells, 'bits', split_axis=1, concat_axis=0, tiled=True)  15.4 us
    dot_general x4, matrix products, one_group(): jnp.einsum('dcph,dpl->dhl', left, low_onehot, preferred_element_type=jnp....  14.9 us
    reshape x2, local copies, waits for them, and re-layouts, build_filter(): jnp.broadcast_to(element_weights[:, :, None], (doc_count, elem_count, HAS...  12.4 us
    convert_element_type x4, other arithmetic, one_group(): (high_block[:, :, None] == jnp.arange(high_cells, dtype=jnp.int32)).astyp...  12.2 us
    all_to_all x1, starting transfers between devices, body(): lax.all_to_all(pair_cells, 'bits', split_axis=1, concat_axis=0, tiled=True)  8.26 us
    all_to_all x1, starting transfers between devices, body(): lax.all_to_all(picked_cells, 'bits', split_axis=0, concat_axis=2, tiled=T...  3.94 us
  transfers between devices with their start and end apart: 2, of which 1 were waited for; matrix products, arithmetic and copies ran while one was open for 2% of the time, Pallas kernels for 0%

commit v1 on v0

--- a/solution.py
+++ b/solution.py
@@ -95,7 +95,9 @@
         lax.all_gather(set_sizes.astype(jnp.float32), ("bits", "docs"), axis=0, tiled=True),
     )
     pair_cells = lax.all_gather(own_cells, "docs", axis=0, tiled=True)
-    slice_cells = lax.all_to_all(pair_cells, "bits", split_axis=1, concat_axis=0, tiled=True)
+    pieces = jnp.split(pair_cells, lax.axis_size("bits"), axis=1)
+    received = lax.all_to_all(jnp.stack(pieces), "bits", 0, 0)
+    slice_cells = jnp.concatenate(received, axis=0)
     tile_rows = row_group * row_half + (candidates[0][:, :, None] * TILE + tile_offsets).reshape(
         blocks, slot_count
     )

time: 159 us -> 168 us (1.057)
  local copies, waits for them, and re-layouts: 21 us -> 29.9 us
    unnamed x12 -> x27, local copies, waits for them, and re-layouts: 1.3 us -> 10.4 us
where the time goes in v1:
time: 168 us; the launch traced here: 167 us
  blocking collectives  47.1 us (28%)
  other arithmetic  45.5 us (27%)
  local copies, waits for them, and re-layouts  29.9 us (18%)
  matrix products  16.3 us (10%)
  waiting for transfers between devices  15.4 us (9%)
  starting transfers between devices  12.2 us (7%)
    unnamed x1, blocking collectives  44.8 us
    reduce_sum x4, other arithmetic, one_group(): jnp.einsum('dcph,dpl->dhl', left, low_onehot, preferred_element_type=jnp....  31.4 us
    all_to_all x1, waiting for transfers between devices, body(): received = lax.all_to_all(jnp.stack(pieces), 'bits', 0, 0)  15.4 us
    dot_general x4, matrix products, one_group(): jnp.einsum('dcph,dpl->dhl', left, low_onehot, preferred_element_type=jnp....  14.9 us
    reshape x2, local copies, waits for them, and re-layouts, build_filter(): jnp.broadcast_to(element_weights[:, :, None], (doc_count, elem_count, HAS...  12.4 us
    convert_element_type x4, other arithmetic, one_group(): (high_block[:, :, None] == jnp.arange(high_cells, dtype=jnp.int32)).astyp...  12.2 us
    unnamed x27, local copies, waits for them, and re-layouts  10.4 us
    all_to_all x1, starting transfers between devices, body(): received = lax.all_to_all(jnp.stack(pieces), 'bits', 0, 0)  8.26 us
  transfers between devices with their start and end apart: 2, of which 1 were waited for; matrix products, arithmetic and copies ran while one was open for 2% of the time, Pallas kernels for 0%

profile of v1, /device:TPU:0, one launch (start us, length us, event | category | flops | bytes accessed | tf_op | source)
XLA Modules:
  0.0 166.8 jit_solution(14337301838698218462)
XLA Ops:
  0.0 1.1 copy.28
  1.5 5.7 %reshape.168 = f32[4,8,1,4096]{1,0,3,2:T(4,128)} reshape(f32[32,1024,4]{0,2,1:T(4,128)S(1)} %broadcast_in_dim.12) | data formatting | bytes 1048576 | tf_op jit(solution)/shard_map/reshape | solution.py:19
  7.2 6.7 %copy.29 = f32[4,8,1,4096]{3,1,2,0:T(8,128)S(1)} copy(f32[4,8,1,4096]{1,0,3,2:T(4,128)} %reshape.168) | data formatting | bytes 1048576 | tf_op jit(solution)/shard_map/reshape | solution.py:19
  14.7 60.3 %while.10 = (s32[]{:T(128)}, bf16[4,8,4096]{2,1,0:T(8,128)(2,1)S(1)}, bf16[4,8,3,4096]{3,1,2,0:T(8,128)(2,1)S(1)}, s32[4,8,4096]{2,1,0:T(8,128)S(1)}, s32[4,8,4096]{2,1,0:T(8,128)S(1)}, /*index=5*/s32[]{:T(128)}) while((s32[]{:T(128)}, bf16[4,8,4096]{2,1,0:T(8,128)(2,1)S(1)}, bf16[4,8,3,4096]{3,1,2,0:T(8,128)(2,1)S(1)}, ...), condition=%wide.region_2.3_spmd, body=%wide.region_0.2_spmd.sunk | while | flops 304087040 | bytes 18874448 | solution.py:44
  14.8 3.0 %fusion.39 = bf16[8,4096,64]{1,2,0:T(8,128)(2,1)} fusion(s32[8,4096]{1,0:T(8,128)S(1)} %get-tuple-element.109), kind=kLoop, calls=%fused_computation.5.clone.1 | loop fusion | flops 4194304 | bytes 4325376 | tf_op jit(solution)/shard_map/while/body/eval_jaxpr/convert_element_type | solution.py:34
  18.0 7.9 %convert_reduce_fusion.2 = bf16[8,4096,64]{1,2,0:T(8,128)(2,1)} fusion(bf16[8,4096,64]{1,2,0:T(8,128)(2,1)} %fusion.39, bf16[8,3,4096]{2,1,0:T(4,128)(2,1)S(1)} %bitcast.109), kind=kLoop, calls=%fused_computation.2.clone.1 | loop fusion | flops 29360128 | bytes 8585216 | tf_op jit(solution)/shard_map/while/body/eval_jaxpr/dcph,dpl->dhl/reduce_sum | solution.py:41
  25.9 3.7 %fusion.40 = bf16[8,64,64]{2,1,0:T(8,128)(2,1)S(1)} fusion(bf16[8,4096,64]{1,2,0:T(8,128)(2,1)} %convert_reduce_fusion.2, s32[8,4096]{1,0:T(8,128)S(1)} %get-tuple-element.110), kind=kOutput, calls=%fused_computation.6.clone.1 | convolution fusion | flops 270532608 | bytes 4390912 | tf_op jit(solution)/shard_map/while/body/eval_jaxpr/dcph,dpl->dhl/dot_general | solution.py:41
  29.8 3.0 %fusion.39 = bf16[8,4096,64]{1,2,0:T(8,128)(2,1)} fusion(s32[8,4096]{1,0:T(8,128)S(1)} %get-tuple-element.109), kind=kLoop, calls=%fused_computation.5.clone.1 | loop fusion | flops 4194304 | bytes 4325376 | tf_op jit(solution)/shard_map/while/body/eval_jaxpr/convert_element_type | solution.py:34
  33.1 7.9 %convert_reduce_fusion.2 = bf16[8,4096,64]{1,2,0:T(8,128)(2,1)} fusion(bf16[8,4096,64]{1,2,0:T(8,128)(2,1)} %fusion.39, bf16[8,3,4096]{2,1,0:T(4,128)(2,1)S(1)} %bitcast.109), kind=kLoop, calls=%fused_computation.2.clone.1 | loop fusion | flops 29360128 | bytes 8585216 | tf_op jit(solution)/shard_map/while/body/eval_jaxpr/dcph,dpl->dhl/reduce_sum | solution.py:41
  40.9 3.7 %fusion.40 = bf16[8,64,64]{2,1,0:T(8,128)(2,1)S(1)} fusion(bf16[8,4096,64]{1,2,0:T(8,128)(2,1)} %convert_reduce_fusion.2, s32[8,4096]{1,0:T(8,128)S(1)} %get-tuple-element.110), kind=kOutput, calls=%fused_computation.6.clone.1 | convolution fusion | flops 270532608 | bytes 4390912 | tf_op jit(solution)/shard_map/while/body/eval_jaxpr/dcph,dpl->dhl/dot_general | solution.py:41
  44.9 3.0 %fusion.39 = bf16[8,4096,64]{1,2,0:T(8,128)(2,1)} fusion(s32[8,4096]{1,0:T(8,128)S(1)} %get-tuple-element.109), kind=kLoop, calls=%fused_computation.5.clone.1 | loop fusion | flops 4194304 | bytes 4325376 | tf_op jit(solution)/shard_map/while/body/eval_jaxpr/convert_element_type | solution.py:34
  48.1 7.9 %convert_reduce_fusion.2 = bf16[8,4096,64]{1,2,0:T(8,128)(2,1)} fusion(bf16[8,4096,64]{1,2,0:T(8,128)(2,1)} %fusion.39, bf16[8,3,4096]{2,1,0:T(4,128)(2,1)S(1)} %bitcast.109), kind=kLoop, calls=%fused_computation.2.clone.1 | loop fusion | flops 29360128 | bytes 8585216 | tf_op jit(solution)/shard_map/while/body/eval_jaxpr/dcph,dpl->dhl/reduce_sum | solution.py:41
  56.0 3.7 %fusion.40 = bf16[8,64,64]{2,1,0:T(8,128)(2,1)S(1)} fusion(bf16[8,4096,64]{1,2,0:T(8,128)(2,1)} %convert_reduce_fusion.2, s32[8,4096]{1,0:T(8,128)S(1)} %get-tuple-element.110), kind=kOutput, calls=%fused_computation.6.clone.1 | convolution fusion | flops 270532608 | bytes 4390912 | tf_op jit(solution)/shard_map/while/body/eval_jaxpr/dcph,dpl->dhl/dot_general | solution.py:41
  60.0 3.0 %fusion.39 = bf16[8,4096,64]{1,2,0:T(8,128)(2,1)} fusion(s32[8,4096]{1,0:T(8,128)S(1)} %get-tuple-element.109), kind=kLoop, calls=%fused_computation.5.clone.1 | loop fusion | flops 4194304 | bytes 4325376 | tf_op jit(solution)/shard_map/while/body/eval_jaxpr/convert_element_type | solution.py:34
  63.2 7.9 %convert_reduce_fusion.2 = bf16[8,4096,64]{1,2,0:T(8,128)(2,1)} fusion(bf16[8,4096,64]{1,2,0:T(8,128)(2,1)} %fusion.39, bf16[8,3,4096]{2,1,0:T(4,128)(2,1)S(1)} %bitcast.109), kind=kLoop, calls=%fused_computation.2.clone.1 | loop fusion | flops 29360128 | bytes 8585216 | tf_op jit(solution)/shard_map/while/body/eval_jaxpr/dcph,dpl->dhl/reduce_sum | solution.py:41
  71.1 3.7 %fusion.40 = bf16[8,64,64]{2,1,0:T(8,128)(2,1)S(1)} fusion(bf16[8,4096,64]{1,2,0:T(8,128)(2,1)} %convert_reduce_fusion.2, s32[8,4096]{1,0:T(8,128)S(1)} %get-tuple-element.110), kind=kOutput, calls=%fused_computation.6.clone.1 | convolution fusion | flops 270532608 | bytes 4390912 | tf_op jit(solution)/shard_map/while/body/eval_jaxpr/dcph,dpl->dhl/dot_general | solution.py:41
  75.0 2.3 %all_gather.9 = bf16[64,4096]{1,0:T(8,128)(2,1)S(1)} all-gather(bf16[32,4096]{1,0:T(8,128)(2,1)S(1)} %bitcast.110), channel_id=1, replica_groups=mesh['bits'=16,'docs'=2] {'docs'}, dimensions={0}, use_global_device_ids=true | all-gather | bytes 786432 | tf_op jit(solution)/shard_map/all_gather | solution.py:97
  77.3 0.6 fusion.29
  78.5 0.6 fusion.27
  79.7 0.6 fusion.25
  81.0 0.6 fusion.23
  82.8 0.6 fusion.20
  83.4 0.6 fusion.19
  87.0 8.3 %all-to-all-start = ((bf16[16,64,256]{2,1,0:T(8,128)(2,1)}), bf16[16,64,256]{2,1,0:T(8,128)(2,1)S(1)}, u32[]{:S(2)}, u32[]{:S(2)}) async-start(bf16[16,64,256]{2,1,0:T(8,128)(2,1)} %fusion.14), calls=%async_computation | async-start | bytes 1048576 | tf_op jit(solution)/shard_map/all_to_all | solution.py:99
  95.3 15.4 %all-to-all-done = bf16[16,64,256]{2,1,0:T(8,128)(2,1)S(1)} async-done(((bf16[16,64,256]{2,1,0:T(8,128)(2,1)}), bf16[16,64,256]{2,1,0:T(8,128)(2,1)S(1)}, u32[]{:S(2)}, u32[]{:S(2)}) %all-to-all-start) | async-done | bytes 524320 | tf_op jit(solution)/shard_map/all_to_all | solution.py:99
  111.9 1.3 copy.31
  113.3 3.9 %all-to-all-start.1 = ((bf16[16,128,256]{1,2,0:T(8,128)(2,1)}), bf16[16,128,256]{1,2,0:T(8,128)(2,1)S(1)}, u32[]{:S(2)}, u32[]{:S(2)}) async-start(bf16[16,128,256]{1,2,0:T(8,128)(2,1)} %copy.31), calls=%async_computation.1 | async-start | bytes 2097152 | tf_op jit(solution)/shard_map/all_to_all | solution.py:105
  117.8 44.8 %all-reduce.2 = (f32[1024]{0:T(1024)S(1)}, f32[1024]{0:T(1024)S(1)}) all-reduce(f32[1024]{0:T(1024)S(1)} %convert_dynamic-update-slice_fusion, f32[1024]{0:T(1024)S(1)} %dynamic-update-slice), channel_id=1, replica_groups=mesh['bits'=16,'docs'=2] {'bits','docs'}, use_global_device_ids=true, to_apply=%add.1 | all-reduce | flops 2048 | bytes 16384
  163.1 1.0 gather_fusion
  164.1 1.0 gather_fusion.1
  165.1 0.8 bitcast_multiply_fusion
  165.9 1.0 divide_bitcast_fusion
  (66 shorter events, 11.1 us)
Async XLA Ops:
  7.2 6.7 %copy-start.3 = (s32[32]{0:T(128)S(1)}, s32[32]{0:T(128)}, u32[]{:S(2)}) copy-start(s32[32]{0:T(128)} %param.9) | copy-start | bytes 388
  7.2 7.1 %copy-start = (s32[32,4096]{1,0:T(8,128)S(1)}, s32[32,4096]{1,0:T(8,128)}, u32[]{:S(2)}) copy-start(s32[32,4096]{1,0:T(8,128)} %param.7) | copy-start | bytes 1572868
  14.7 96.2 %copy-start.2 = (s32[1,16,16]{2,1,0:T(8,128)S(1)}, s32[1,16,16]{2,1,0:T(8,128)}, u32[]{:S(2)}) copy-start(s32[1,16,16]{2,1,0:T(8,128)} %param.11) | copy-start | bytes 3076
  87.0 23.6 %all-to-all-start = ((bf16[16,64,256]{2,1,0:T(8,128)(2,1)}), bf16[16,64,256]{2,1,0:T(8,128)(2,1)S(1)}, u32[]{:S(2)}, u32[]{:S(2)}) async-start(bf16[16,64,256]{2,1,0:T(8,128)(2,1)} %fusion.14), calls=%async_computation | async-start | bytes 1048576 | tf_op jit(solution)/shard_map/all_to_all | solution.py:99
  95.3 21.9 %copy-start.1 = (bf16[4096]{0:T(1024)(128)(2,1)S(1)}, bf16[4096]{0:T(1024)(128)(2,1)}, u32[]{:S(2)}) copy-start(bf16[4096]{0:T(1024)(128)(2,1)} %param.10) | copy-start | bytes 24580
  113.3 51.8 %all-to-all-start.1 = ((bf16[16,128,256]{1,2,0:T(8,128)(2,1)}), bf16[16,128,256]{1,2,0:T(8,128)(2,1)S(1)}, u32[]{:S(2)}, u32[]{:S(2)}) async-start(bf16[16,128,256]{1,2,0:T(8,128)(2,1)} %copy.31), calls=%async_computation.1 | async-start | bytes 2097152 | tf_op jit(solution)/shard_map/all_to_all | solution.py:105
